TPU v7x, 128 devices: a whole 4x4x4 slice. The times are simulated.
128 devices in a mesh: dom: 64 (over z_hi, x, y, core), grp: 2 (over z_lo).
Axes of the slice: x: 4, y: 4, z: 4 (z_hi: 2, z_lo: 2; z = z_hi * 2 + z_lo), core: 2. Of those that a mesh axis runs over, the one named last changes fastest.
Arguments:
- node_features: bfloat16 [1048576, 256], P(('dom', 'grp')), may hold values from -6 to 6
- vertex_count: int32 [128], P(('dom', 'grp')), may hold values from 4096 to 8192, as said below
- send_rows: int32 [128, 2, 2048], P(('dom', 'grp')), may hold values from 0 to 8191, as said below
- block_values: bfloat16 [8192, 4, 128, 128], P(('dom', 'grp')), may hold values from -0.25 to 0.25
- block_cols: int32 [8192, 4], P(('dom', 'grp')), may hold values from 0 to 95
- block_count: int32 [8192], P(('dom', 'grp')), may hold values from 1 to 4
- w_query: bfloat16 [2, 256, 256], replicated, may hold values from -0.375 to 0.375
- w_key: bfloat16 [2, 256, 256], replicated, may hold values from -0.375 to 0.375
- w_value: bfloat16 [2, 256, 256], replicated, may hold values from -0.375 to 0.375
- w_message: bfloat16 [2, 256, 256], replicated, may hold values from -0.375 to 0.375
- w_out: bfloat16 [2, 256, 256], replicated, may hold values from -0.375 to 0.375
- attn_gain: float32 [2, 256], replicated, may hold values from 0.25 to 1.75
Outputs:
- updated: bfloat16 [1048576, 256], P(('dom', 'grp'))
Inputs may be any that keep to these rules, and one draw needn't show every extreme that they name: Rows of partition p at local index vertex_count[p] or above are padding; some partition uses all 8192 slots. send_rows[p, 0, :] and send_rows[p, 1, :] each list 2048 distinct local rows of partition p below vertex_count[p]. `block_cols`: extended tiles below 64 are the partition's own; the next 16 come from the lower neighbour, the last 16 from the upper one. Only the first block_count[g] blocks of row tile g are used.
All inputs are finite; a program needn't handle non-finite values.
Results may differ from a plain program's by a relative error of at most 0.0063.
Values may be sent and summed in bfloat16 or wider, within the bound.
A program may use at most 128 MiB of HBM per device.

v0:
```python
import jax
import jax.numpy as jnp
from jax import lax
from jax.sharding import PartitionSpec as P

epsilon = 1e-06


def extended_2(block, sides, width):
    for axis, dim in sides:
        count = lax.axis_size(axis)
        forward = [(i, i + 1) for i in range(count - 1)]
        backward = [(target, source) for source, target in forward]
        low = lax.ppermute(
            lax.slice_in_dim(block, block.shape[dim] - width, None, axis=dim), axis, forward
        )
        high = lax.ppermute(lax.slice_in_dim(block, 0, width, axis=dim), axis, backward)
        block = jnp.concatenate([low, block, high], axis=dim)
    return block


def feature_map(inputs):
    return jax.nn.elu(inputs) + 1.0


def on_device(
    node_features,
    vertex_count,
    send_rows,
    block_values,
    block_cols,
    block_count,
    w_query,
    w_key,
    w_value,
    w_message,
    w_out,
    attn_gain,
):
    vertices, feat_width = node_features.shape
    block_slots = block_values.shape[1]
    tile_rows = block_values.shape[2]
    positions = jnp.arange(vertices, dtype=jnp.int32)
    keep_rows = (positions < vertex_count[0])[:, None]
    hidden = jnp.where(keep_rows, node_features, jnp.zeros_like(node_features))
    live_slots = jnp.arange(block_slots, dtype=jnp.int32)[None, :] < block_count[:, None]
    used_blocks = jnp.where(
        live_slots[:, :, None, None], block_values, jnp.zeros_like(block_values)
    )
    for layer_num in range(w_query.shape[0]):
        projected = feature_map(
            jnp.dot(hidden, w_key[layer_num], preferred_element_type=jnp.float32)
        )
        key_rows = jnp.where(keep_rows, projected, jnp.zeros_like(projected)).astype(jnp.bfloat16)
        value_rows = jnp.dot(hidden, w_value[layer_num], preferred_element_type=jnp.float32).astype(
            jnp.bfloat16
        )
        partial_value = lax.dot_general(
            key_rows, value_rows, (((0,), (0,)), ((), ())), preferred_element_type=jnp.float32
        )
        query_rows = feature_map(
            jnp.dot(hidden, w_query[layer_num], preferred_element_type=jnp.float32)
        ).astype(jnp.bfloat16)
        summary_cast = lax.psum(partial_value, ("dom", "grp")).astype(jnp.bfloat16)
        mixed_rows = jnp.dot(query_rows, summary_cast, preferred_element_type=jnp.float32)
        outgoing = hidden[send_rows[0]]
        padded = extended_2(outgoing, ((("dom", "grp"), 0),), 1)
        lower_rows = padded[0]
        upper_rows = padded[3]
        extended = jnp.concatenate([hidden, lower_rows, upper_rows], axis=0)
        extended = extended.reshape(-1, tile_rows, feat_width)
        picked = extended[block_cols]
        aggregated = jnp.einsum(
            "tjab,tjbd->tad", used_blocks, picked, preferred_element_type=jnp.float32
        )
        aggregated = aggregated.reshape(vertices, feat_width).astype(jnp.bfloat16)
        message = jax.nn.silu(
            jnp.dot(aggregated, w_message[layer_num], preferred_element_type=jnp.float32)
        )
        scale = lax.rsqrt(jnp.mean(mixed_rows * mixed_rows, axis=-1, keepdims=True) + epsilon)
        attended = (mixed_rows * scale * attn_gain[layer_num][None, :]).astype(jnp.bfloat16)
        output = jnp.dot(attended, w_out[layer_num], preferred_element_type=jnp.float32)
        renewed = hidden.astype(jnp.float32) + message + output
        hidden = jnp.where(keep_rows, renewed, jnp.zeros_like(renewed)).astype(jnp.bfloat16)
    return hidden


def solution(mesh):
    placed = (
        P(("dom", "grp"), None),
        P(("dom", "grp")),
        P(("dom", "grp"), None, None),
        P(("dom", "grp"), None, None, None),
        P(("dom", "grp"), None),
        P(("dom", "grp")),
        P(),
        P(),
        P(),
        P(),
        P(),
        P(),
    )
    return jax.shard_map(
        on_device, mesh=mesh, in_specs=placed, out_specs=P(("dom", "grp"), None), check_vma=False
    )
```

profile of v0, /device:TPU:1, one launch (start us, length us, event | category | flops | bytes accessed | tf_op | source)
XLA Modules:
  0.0 396.0 jit_solution(15581483642133797909)
XLA Ops:
  0.7 0.7 fusion.82
  1.4 5.2 %broadcast_select_fusion.3 = bf16[8192,256]{1,0:T(8,128)(2,1)} fusion(bf16[8192,256]{1,0:T(8,128)(2,1)} %param.12, pred[8192]{0:T(1024)(128)(4,1)S(1)} %iota_compare_fusion.1), kind=kLoop, calls=%fused_computation.61 | loop fusion | flops 2097152 | bytes 8396800 | tf_op jit(solution)/shard_map/jit(_where)/select_n | solution.py:45
  6.7 15.8 %gather_fusion = bf16[4096,256]{1,0:T(8,128)(2,1)S(1)} fusion(bf16[8192,256]{1,0:T(8,128)(2,1)} %broadcast_select_fusion.3, s32[4096]{0:T(1024)S(1)} %broadcast_clamp_fusion), kind=kCustom, calls=%fused_computation | custom fusion | bytes 4210688 | tf_op jit(solution)/shard_map/gather | solution.py:66
  22.4 1.2 slice_bitcast_fusion.3
  23.6 4.9 %collective-permute-start.1 = (bf16[1,2048,256]{2,1,0:T(8,128)(2,1)}, bf16[1,2048,256]{2,1,0:T(8,128)(2,1)S(1)}, u32[]{:S(2)}, u32[]{:S(2)}) collective-permute-start(bf16[1,2048,256]{2,1,0:T(8,128)(2,1)} %get-tuple-element.8), channel_id=1, source_target_pairs={{1,0},{2,1},{3,2},{4,3},{5,4},{6,5},{7,6},{8,7},{9,8},{10,9},{11,1... | collective-permute-start | bytes 3145736 | tf_op jit(solution)/shard_map/ppermute | solution.py:17
  28.6 1.9 collective-permute-start
  30.5 0.0 copy-done.7
  30.5 0.1 copy.13
  30.6 0.1 reshape.91
  30.7 0.0 copy-done.9
  30.7 0.1 iota_compare_fusion
  30.8 0.0 copy-done.2
  30.8 0.0 copy-start.5
  30.8 6.7 %fusion.56 = f32[8192,256]{1,0:T(8,128)} fusion(bf16[8192,256]{1,0:T(8,128)(2,1)} %broadcast_select_fusion.3, bf16[2,256,256]{2,1,0:T(8,128)(2,1)S(1)} %copy-done.2), kind=kOutput, calls=%fused_computation.76 | convolution fusion | flops 1073741824 | bytes 12713984 | tf_op jit(solution)/shard_map/dot_general | solution.py:52
  37.5 10.7 %fusion.36 = f32[256,256]{1,0:T(8,128)} fusion(f32[8192,256]{1,0:T(8,128)} %fusion.56, pred[8192]{0:T(1024)(128)(4,1)S(1)} %iota_compare_fusion.1, bf16[8192,256]{1,0:T(8,128)(2,1)} %broadcast_select_fusion.3, bf16[2,256,256]{2,1,0:T(8,128)(2,1)} %param.20), kind=kOutput, calls=%fused_computation.58 | convolution fusion | flops 2162163712 | bytes 12984320 | tf_op jit(solution)/shard_map/dot_general | solution.py:58
  48.2 84.7 %all-reduce.2 = bf16[256,256]{1,0:T(8,128)(2,1)} all-reduce(f32[256,256]{1,0:T(8,128)} %fusion.36), channel_id=1, replica_groups=mesh['dom'=64,'grp'=2] {'dom','grp'}, use_global_device_ids=true, to_apply=%region_0.1 | all-reduce | flops 65536 | bytes 393216 | tf_op jit(solution)/shard_map/psum | solution.py:64
  132.9 0.0 copy-done.8
  132.9 10.0 %multiply_reduce_fusion.1 = (f32[8192]{0:T(1024)S(1)}, f32[8192,256]{0,1:T(8,128)}) fusion(bf16[256,256]{1,0:T(8,128)(2,1)} %all-reduce.2, bf16[8192,256]{1,0:T(8,128)(2,1)} %broadcast_select_fusion.3, bf16[2,256,256]{2,1,0:T(8,128)(2,1)} %param.18), kind=kOutput, calls=%fused_computation.39 | convolution fusion | flops 2162155520 | bytes 12877824 | tf_op jit(solution)/shard_map/dot_general | solution.py:65
  143.0 0.0 collective-permute-done.1
  143.0 0.0 collective-permute-done
  143.0 18.8 %pad_maximum_fusion = bf16[12288,256]{1,0:T(8,128)(2,1)} fusion(bf16[2048,256]{1,0:T(8,128)(2,1)S(1)} %bitcast.96, bf16[2048,256]{1,0:T(8,128)(2,1)S(1)} %bitcast.97, bf16[8192,256]{1,0:T(8,128)(2,1)} %broadcast_select_fusion.3), kind=kLoop, calls=%fused_computation.43 | loop fusion | flops 18874368 | bytes 12582912 | tf_op jit(solution)/shard_map/concatenate | solution.py:70
  161.8 13.0 %gather_fusion.1 = bf16[256,128,256]{2,1,0:T(8,128)(2,1)} fusion(bf16[96,128,256]{2,1,0:T(8,128)(2,1)} %bitcast.91, s32[1024]{0:T(1024)S(1)} %pad_clamp_fusion), kind=kCustom, calls=%fused_computation.1 | custom fusion | bytes 33555456 | tf_op jit(solution)/shard_map/gather | solution.py:72
  174.8 0.0 copy-done.5
  174.8 12.6 %bitcast_convert_fusion.1 = bf16[64,128,256]{2,1,0:T(8,128)(2,1)} fusion(bf16[64,4,128,256]{3,2,1,0:T(8,128)(2,1)} %bitcast.93, bf16[64,4,128,128]{3,2,1,0:T(8,128)(2,1)} %param.15, pred[64,4]{1,0:T(8,128)(4,1)S(1)} %iota_compare_fusion), kind=kOutput, calls=%fused_computation.35 | convolution fusion | flops 2153775104 | bytes 29360384 | tf_op jit(solution)/shard_map/tjab,tjbd->tad/dot_general | solution.py:73
  187.4 0.0 copy-done.3
  187.4 3.6 fusion.64
  191.0 0.0 copy-done
  191.0 0.0 copy-done.10
  191.0 9.0 %fusion.2 = bf16[8192,256]{1,0:T(8,128)(2,1)} fusion(f32[8192,256]{1,0:T(8,128)S(1)} %fusion.64, bf16[8192,256]{1,0:T(8,128)(2,1)S(1)} %copy-done, f32[8192,256]{0,1:T(8,128)} %get-tuple-element.12, f32[256]{0:T(256)S(1)} %bitcast.102, f32[8192]{0:T(1024)S(1)} %add_rsqrt_fusion.1, pred[8192]{0:T(1024)(128)(4,1)S(1)} %iota_compare_fusion.1, ...), kind=kOutput, calls=%fused_computation.16 | convolution fusion | flops 1098907648 | bytes 25338880 | tf_op jit(solution)/shard_map/dot_general | solution.py:82
  200.0 15.7 %gather_fusion.2 = bf16[4096,256]{1,0:T(8,128)(2,1)S(1)} fusion(bf16[8192,256]{1,0:T(8,128)(2,1)} %fusion.2, s32[4096]{0:T(1024)S(1)} %broadcast_clamp_fusion), kind=kCustom, calls=%fused_computation.2 | custom fusion | bytes 4210688 | tf_op jit(solution)/shard_map/gather | solution.py:66
  215.8 6.7 %fusion.43 = f32[8192,256]{1,0:T(8,128)} fusion(bf16[8192,256]{1,0:T(8,128)(2,1)} %fusion.2, bf16[2,256,256]{2,1,0:T(8,128)(2,1)S(1)} %copy-done.2), kind=kOutput, calls=%fused_computation.68 | convolution fusion | flops 1073741824 | bytes 12713984 | tf_op jit(solution)/shard_map/dot_general | solution.py:52
  222.4 1.2 slice_bitcast_fusion.1
  223.6 3.8 collective-permute-start.3
  227.4 1.9 collective-permute-start.2
  229.3 10.0 %fusion.34 = f32[256,256]{1,0:T(8,128)S(1)} fusion(f32[8192,256]{1,0:T(8,128)} %fusion.43, pred[8192]{0:T(1024)(128)(4,1)S(1)} %iota_compare_fusion.1, bf16[8192,256]{1,0:T(8,128)(2,1)} %fusion.2, bf16[2,256,256]{2,1,0:T(8,128)(2,1)} %param.20), kind=kOutput, calls=%fused_computation.57 | convolution fusion | flops 2162163712 | bytes 12984320 | tf_op jit(solution)/shard_map/dot_general | solution.py:58
  239.3 89.6 %all-reduce.3 = bf16[256,256]{1,0:T(8,128)(2,1)S(1)} all-reduce(f32[256,256]{1,0:T(8,128)S(1)} %fusion.34), channel_id=1, replica_groups=mesh['dom'=64,'grp'=2] {'dom','grp'}, use_global_device_ids=true, to_apply=%region_2.3 | all-reduce | flops 65536 | bytes 393216 | tf_op jit(solution)/shard_map/psum | solution.py:64
  328.9 9.9 %multiply_reduce_fusion = (f32[8192]{0:T(1024)S(1)}, f32[8192,256]{0,1:T(8,128)}) fusion(bf16[256,256]{1,0:T(8,128)(2,1)S(1)} %all-reduce.3, bf16[8192,256]{1,0:T(8,128)(2,1)} %fusion.2, bf16[2,256,256]{2,1,0:T(8,128)(2,1)} %param.18), kind=kOutput, calls=%fused_computation.37 | convolution fusion | flops 2162155520 | bytes 12877824 | tf_op jit(solution)/shard_map/dot_general | solution.py:65
  338.9 0.0 collective-permute-done.3
  338.9 0.0 collective-permute-done.2
  338.9 18.8 %pad_maximum_fusion.1 = bf16[12288,256]{1,0:T(8,128)(2,1)} fusion(bf16[2048,256]{1,0:T(8,128)(2,1)S(1)} %bitcast.98, bf16[2048,256]{1,0:T(8,128)(2,1)S(1)} %bitcast.99, bf16[8192,256]{1,0:T(8,128)(2,1)} %fusion.2), kind=kLoop, calls=%fused_computation.44 | loop fusion | flops 18874368 | bytes 12582912 | tf_op jit(solution)/shard_map/concatenate | solution.py:70
  357.7 12.8 %gather_fusion.3 = bf16[256,128,256]{2,1,0:T(8,128)(2,1)} fusion(bf16[96,128,256]{2,1,0:T(8,128)(2,1)} %bitcast.90, s32[1024]{0:T(1024)S(1)} %pad_clamp_fusion), kind=kCustom, calls=%fused_computation.3 | custom fusion | bytes 33555456 | tf_op jit(solution)/shard_map/gather | solution.py:72
  370.5 0.0 copy-done.6
  370.5 12.6 %bitcast_convert_fusion = bf16[64,128,256]{2,1,0:T(8,128)(2,1)} fusion(bf16[64,4,128,256]{3,2,1,0:T(8,128)(2,1)} %bitcast.92, bf16[64,4,128,128]{3,2,1,0:T(8,128)(2,1)} %param.15, pred[64,4]{1,0:T(8,128)(4,1)S(1)} %copy-done.6), kind=kOutput, calls=%fused_computation.34 | convolution fusion | flops 2153775104 | bytes 29360384 | tf_op jit(solution)/shard_map/tjab,tjbd->tad/dot_general | solution.py:73
  383.1 0.0 copy-done.4
  383.1 3.6 fusion.51
  386.7 0.0 copy-done.1
  386.7 0.0 copy-done.11
  386.7 9.0 %fusion.3 = bf16[8192,256]{1,0:T(8,128)(2,1)} fusion(f32[8192,256]{1,0:T(8,128)S(1)} %fusion.51, bf16[8192,256]{1,0:T(8,128)(2,1)S(1)} %copy-done.1, f32[8192,256]{0,1:T(8,128)} %get-tuple-element.14, f32[256]{0:T(256)S(1)} %bitcast.101, f32[8192]{0:T(1024)S(1)} %add_rsqrt_fusion, pred[8192]{0:T(1024)(128)(4,1)S(1)} %iota_compare_fusion.1, ...), kind=kOutput, calls=%fused_computation.17 | convolution fusion | flops 1098907648 | bytes 25338880 | tf_op jit(solution)/shard_map/dot_general | solution.py:82
  (19 shorter events, 0.1 us)
Async XLA Ops:
  6.7 23.8 %copy-start.7 = (s32[64,4]{0,1:T(4,128)S(1)}, s32[64,4]{0,1:T(4,128)}, u32[]{:S(2)}) copy-start(s32[64,4]{0,1:T(4,128)} %param.16) | copy-start | bytes 3076
  6.7 24.1 %copy-start.9 = (s32[64]{0:T(128)S(1)}, s32[64]{0:T(128)}, u32[]{:S(2)}) copy-start(s32[64]{0:T(128)} %param.17) | copy-start | bytes 772
  6.7 24.1 %copy-start.2 = (bf16[2,256,256]{2,1,0:T(8,128)(2,1)S(1)}, bf16[2,256,256]{2,1,0:T(8,128)(2,1)}, u32[]{:S(2)}) copy-start(bf16[2,256,256]{2,1,0:T(8,128)(2,1)} %param.19) | copy-start | bytes 786436
  23.6 119.3 %collective-permute-start.1 = (bf16[1,2048,256]{2,1,0:T(8,128)(2,1)}, bf16[1,2048,256]{2,1,0:T(8,128)(2,1)S(1)}, u32[]{:S(2)}, u32[]{:S(2)}) collective-permute-start(bf16[1,2048,256]{2,1,0:T(8,128)(2,1)} %get-tuple-element.8), channel_id=1, source_target_pairs={{1,0},{2,1},{3,2},{4,3},{5,4},{6,5},{7,6},{8,7},{9,8},{10,9},{11,1... | collective-permute-start | bytes 3145736 | tf_op jit(solution)/shard_map/ppermute | solution.py:17
  28.6 114.4 %collective-permute-start = (bf16[1,2048,256]{2,1,0:T(8,128)(2,1)S(1)}, bf16[1,2048,256]{2,1,0:T(8,128)(2,1)S(1)}, u32[]{:S(2)}, u32[]{:S(2)}) collective-permute-start(bf16[1,2048,256]{2,1,0:T(8,128)(2,1)S(1)} %get-tuple-element.7), channel_id=1, source_target_pairs={{0,1},{1,2},{2,3},{3,4},{4,5},{5,6},{6,7},{7,8},{8,9},{9,10},{10,1... | collective-permute-start | bytes 3145736 | tf_op jit(solution)/shard_map/ppermute | solution.py:14
  30.8 144.0 %copy-start.5 = (pred[64,4]{1,0:T(8,128)(4,1)}, pred[64,4]{1,0:T(8,128)(4,1)S(1)}, u32[]{:S(2)}) copy-start(pred[64,4]{1,0:T(8,128)(4,1)S(1)} %iota_compare_fusion) | copy-start | bytes 772
  37.5 95.4 %copy-start.8 = (f32[2,256]{1,0:T(2,128)S(1)}, f32[2,256]{1,0:T(2,128)}, u32[]{:S(2)}) copy-start(f32[2,256]{1,0:T(2,128)} %param.23) | copy-start | bytes 6148
  174.8 12.6 %copy-start.3 = (bf16[2,256,256]{2,1,0:T(8,128)(2,1)S(1)}, bf16[2,256,256]{2,1,0:T(8,128)(2,1)}, u32[]{:S(2)}) copy-start(bf16[2,256,256]{2,1,0:T(8,128)(2,1)} %param.21) | copy-start | bytes 786436
  187.4 3.6 copy-start
  187.4 3.6 copy-start.10
  223.6 115.3 %collective-permute-start.3 = (bf16[1,2048,256]{2,1,0:T(8,128)(2,1)}, bf16[1,2048,256]{2,1,0:T(8,128)(2,1)S(1)}, u32[]{:S(2)}, u32[]{:S(2)}) collective-permute-start(bf16[1,2048,256]{2,1,0:T(8,128)(2,1)} %get-tuple-element.6), channel_id=1, source_target_pairs={{1,0},{2,1},{3,2},{4,3},{5,4},{6,5},{7,6},{8,7},{9,8},{10,9},{11,1... | collective-permute-start | bytes 3145736 | tf_op jit(solution)/shard_map/ppermute | solution.py:17
  227.4 111.5 %collective-permute-start.2 = (bf16[1,2048,256]{2,1,0:T(8,128)(2,1)S(1)}, bf16[1,2048,256]{2,1,0:T(8,128)(2,1)S(1)}, u32[]{:S(2)}, u32[]{:S(2)}) collective-permute-start(bf16[1,2048,256]{2,1,0:T(8,128)(2,1)S(1)} %get-tuple-element.5), channel_id=1, source_target_pairs={{0,1},{1,2},{2,3},{3,4},{4,5},{5,6},{6,7},{7,8},{8,9},{9,10},{10,1... | collective-permute-start | bytes 3145736 | tf_op jit(solution)/shard_map/ppermute | solution.py:14
  357.7 12.8 %copy-start.6 = (pred[64,4]{1,0:T(8,128)(4,1)S(1)}, pred[64,4]{1,0:T(8,128)(4,1)}, u32[]{:S(2)}) copy-start(pred[64,4]{1,0:T(8,128)(4,1)} %copy-done.5) | copy-start | bytes 772
  370.5 12.6 %copy-start.4 = (bf16[2,256,256]{2,1,0:T(8,128)(2,1)S(1)}, bf16[2,256,256]{2,1,0:T(8,128)(2,1)}, u32[]{:S(2)}) copy-start(bf16[2,256,256]{2,1,0:T(8,128)(2,1)} %param.21) | copy-start | bytes 786436
  383.1 3.6 copy-start.1
  383.1 3.6 copy-start.11
where the time goes:
time: 403 us; the launch traced here: 396 us
  blocking collectives  174 us (43%)
  matrix products  105 us (26%)
  local copies, waits for them, and re-layouts  59.9 us (15%)
  other arithmetic  43.7 us (11%)
  starting transfers between devices  12.5 us (3%)
    psum x2, blocking collectives, on_device(): summary_cast = lax.psum(partial_value, ('dom', 'grp')).astype(jnp.bfloat16)  174 us
    concatenate x2, other arithmetic, on_device(): extended = jnp.concatenate([hidden, lower_rows, upper_rows], axis=0)  37.6 us
    gather x2, local copies, waits for them, and re-layouts, on_device(): outgoing = hidden[send_rows[0]]  31.5 us
    gather x2, local copies, waits for them, and re-layouts, on_device(): picked = extended[block_cols]  25.8 us
    dot_general x2, matrix products, on_device(): jnp.einsum('tjab,tjbd->tad', used_blocks, picked, preferred_element_type=...  25.2 us
    dot_general x2, matrix products, on_device(): lax.dot_general(key_rows, value_rows, (((0,), (0,)), ((), ())), preferred...  20.8 us
    dot_general x2, matrix products, on_device(): jnp.dot(query_rows, summary_cast, preferred_element_type=jnp.float32)  20 us
    dot_general x2, matrix products, on_device(): jnp.dot(attended, w_out[layer_num], preferred_element_type=jnp.float32)  18.1 us
  transfers between devices with their start and end apart: 4, of which 0 were waited for; matrix products, arithmetic and copies ran while one was open for 12% of the time, Pallas kernels for 0%

commit v1 on v0

v1 whole, which is shorter than its diff:
```python
import functools

import jax
import jax.numpy as jnp
from jax import lax
from jax.experimental import pallas as pl
from jax.experimental.pallas import tpu as pltpu
from jax.sharding import PartitionSpec as P

MESH = pl.DeviceIdType.MESH
epsilon = 1e-06
F32 = jnp.float32
BF16 = jnp.bfloat16

NX, NY, NZ = 4, 4, 4
ROWS = 512
UNROLL = 16
FIRST = 8


def repeat(start, stop, body):
    def step(i, carry):
        body(i)
        return carry

    lax.fori_loop(start, stop, step, 0)


def feature_map(u):
    return jnp.maximum(u, 0.0) + jnp.exp(jnp.minimum(u, 0.0))


def silu(u):
    return 0.5 * u * (1.0 + jnp.tanh(0.5 * u))


def dot(a, b):
    return jnp.dot(a, b, preferred_element_type=F32)


def kernel(
    sizes,
    count_ref,
    rows_ref,
    near_ref,
    far_ref,
    feat_ref,
    blocks_ref,
    wq_ref,
    wk_ref,
    wv_ref,
    wm_ref,
    wo_ref,
    gain_ref,
    out_ref,
    hid,
    halo_0,
    halo_1,
    wide,
    picked,
    send,
    query,
    local,
    res,
    blk,
    summ,
    half,
    quarter,
    piece,
    r1,
    r2,
    r3,
    r4,
    total,
    feat_sem,
    blk_sem,
    out_sem,
    halo_send,
    halo_recv,
    ar_send,
    ar_recv,
):
    layers, vertices, width, tile, slots, halo_rows = sizes
    halos = (halo_0, halo_1)
    tiles = vertices // tile
    side_tiles = halo_rows // tile
    lanes = width // 2
    steps = vertices // ROWS

    dom, grp = lax.axis_index("dom"), lax.axis_index("grp")
    part = dom * 2 + grp
    parts = NX * NY * NZ * 2
    core = lax.rem(dom, 2)
    y = lax.rem(dom // 2, NY)
    x = lax.rem(dom // (2 * NY), NX)
    z = dom // (2 * NY * NX) * 2 + grp

    def place(x_at, y_at, z_at, core_at):
        return {
            "dom": ((z_at // 2 * NX + x_at) * NY + y_at) * 2 + core_at,
            "grp": lax.rem(z_at, 2),
        }

    def place_of(part_at):
        return {"dom": part_at // 2, "grp": lax.rem(part_at, 2)}

    upper = place_of(lax.rem(part + 1, parts))
    lower = place_of(lax.rem(part + parts - 1, parts))
    twin = place(x, y, z, 1 - core)
    x_others = [place(lax.rem(x + k, NX), y, z, core) for k in range(1, NX)]
    y_others = [place(x, lax.rem(y + k, NY), z, core) for k in range(1, NY)]
    z_others = [place(x, y, lax.rem(z + k, NZ), core) for k in range(1, NZ)]

    some_tiles = ROWS // tile

    def hidden(i):
        return hid[pl.ds(i * some_tiles, some_tiles)].reshape(ROWS, width)

    def set_hidden(i, new):
        hid[pl.ds(i * some_tiles, some_tiles)] = new.reshape(some_tiles, tile, width)

    def feat_copy(i):
        at = pl.ds(i * some_tiles, some_tiles)
        return pltpu.make_async_copy(feat_ref.at[at], hid.at[at], feat_sem.at[i])

    def blk_copy(i):
        return pltpu.make_async_copy(blocks_ref.at[i], blk.at[i], blk_sem.at[i])

    for i in range(steps):
        feat_copy(i).start()

    barrier = pltpu.get_barrier_semaphore()
    partners = [upper, lower, twin] + x_others + y_others + z_others
    for partner in partners:
        pl.semaphore_signal(barrier, inc=1, device_id=partner, device_id_type=MESH)

    count = count_ref[0]
    hid[tiles] = jnp.zeros((tile, width), BF16)
    for halo in halos:
        halo[2 * side_tiles] = jnp.zeros((tile, width), BF16)

    def keep(i):
        at = i * ROWS + lax.broadcasted_iota(jnp.int32, (ROWS, width), 0)
        return at < count

    def widen(i, new):
        wide[pl.ds(2 * i * ROWS, ROWS, stride=2), :] = new[:, :lanes]
        wide[pl.ds(2 * i * ROWS + 1, ROWS, stride=2), :] = new[:, lanes:]

    def enter(i):
        feat_copy(i).wait()
        kept = jnp.where(keep(i), hidden(i).astype(F32), 0.0)
        set_hidden(i, kept.astype(BF16))
        widen(i, kept)

    repeat(0, steps, enter)
    repeat(0, tiles, lambda i: blk_copy(i).start())
    pl.semaphore_wait(barrier, len(partners))

    def halo_copy(layer, side, k):
        at = (1 - side) * side_tiles
        return pltpu.make_async_remote_copy(
            src_ref=send.at[side, k],
            dst_ref=halos[layer].at[at + k],
            send_sem=halo_send.at[side, k],
            recv_sem=halo_recv.at[layer, side, k],
            device_id=lower if side == 0 else upper,
            device_id_type=MESH,
        )

    def gather(layer, first, last):
        def chunk(k):
            for side in range(2):
                def some(i):
                    for u in range(UNROLL):
                        at = i * UNROLL + u
                        row = rows_ref[side, k * tile + at]
                        picked[side, pl.ds(2 * at, 2), :] = wide[pl.ds(2 * row, 2), :]

                repeat(0, tile // UNROLL, some)
                send[side, k, :, :lanes] = picked[side, pl.ds(0, tile, stride=2), :].astype(BF16)
                send[side, k, :, lanes:] = picked[side, pl.ds(1, tile, stride=2), :].astype(BF16)
            for side in range(2):
                halo_copy(layer, side, k).start()

        repeat(first, last, chunk)

    def exchange(layer, number, src, dst, target):
        return pltpu.make_async_remote_copy(
            src_ref=src,
            dst_ref=dst,
            send_sem=ar_send.at[layer, number],
            recv_sem=ar_recv.at[layer, number],
            device_id=target,
            device_id_type=MESH,
        )

    def start(copies):
        for copy in copies:
            copy.start()

    def wait(copies):
        for copy in copies:
            copy.wait()

    def blocks_of(t):
        return jnp.concatenate([blk[t, j] for j in range(slots)], axis=1)

    for layer in range(layers):
        wk_t = wk_ref[layer].T
        wv, wq = wv_ref[layer], wq_ref[layer]

        gather(layer, 0, FIRST)

        summ[...] = jnp.zeros_like(summ)

        def add_summary(i):
            h = hidden(i)
            keys = lax.dot_general(wk_t, h, (((1,), (1,)), ((), ())), preferred_element_type=F32)
            keys = feature_map(keys).astype(BF16)
            values = dot(h, wv).astype(BF16)
            summ[...] += dot(keys, values)

        repeat(0, steps, add_summary)

        def ask(i):
            rows = pl.ds(i * ROWS, ROWS)
            query[rows, :] = feature_map(dot(hidden(i), wq)).astype(BF16)

        group = 4

        def gather_local(i):
            for u in range(group):
                t = i * group + u
                if layer == 0:
                    blk_copy(t).wait()
                tiles_here = [hid[near_ref[t * slots + j]] for j in range(slots)]
                local[pl.ds(t * tile, tile), :] = dot(
                    blocks_of(t), jnp.concatenate(tiles_here, axis=0)
                )

        loops = tiles // group

        share = width // 2
        hop = [
            exchange(layer, 0, summ.at[pl.ds((1 - core) * share, share)], r1.at[layer], twin)
        ]
        start(hop)
        repeat(0, steps // 2, ask)
        wait(hop)
        half[...] = summ[pl.ds(core * share, share), :] + r1[layer]

        share //= NX
        hop = [
            exchange(
                layer,
                k,
                half.at[pl.ds(lax.rem(x + k, NX) * share, share)],
                r2.at[layer, k - 1],
                x_others[k - 1],
            )
            for k in range(1, NX)
        ]
        start(hop)
        repeat(steps // 2, steps, ask)
        wait(hop)
        quarter[...] = half[pl.ds(x * share, share), :] + (
            r2[layer, 0] + r2[layer, 1] + r2[layer, 2]
        )

        share //= NY
        hop = [
            exchange(
                layer,
                k + 3,
                quarter.at[pl.ds(lax.rem(y + k, NY) * share, share)],
                r3.at[layer, k - 1],
                y_others[k - 1],
            )
            for k in range(1, NY)
        ]
        start(hop)
        repeat(0, loops // 4, gather_local)
        wait(hop)
        piece[...] = quarter[pl.ds(y * share, share), :] + (
            r3[layer, 0] + r3[layer, 1] + r3[layer, 2]
        )

        hop = [
            exchange(layer, k + 6, piece, r4.at[layer, k - 1], z_others[k - 1])
            for k in range(1, NZ)
        ]
        start(hop)
        gather(layer, FIRST, side_tiles)
        repeat(loops // 4, loops // 2, gather_local)
        wait(hop)
        at = core * (width // 2) + x * (width // 8) + y * share
        total[layer, pl.ds(at, share), :] = piece[...] + (
            r4[layer, 0] + r4[layer, 1] + r4[layer, 2]
        )

        here = total.at[layer, pl.ds(at, share)]
        hop = [
            exchange(layer, k + 9, here, here, y_others[k - 1]) for k in range(1, NY)
        ]
        start(hop)
        repeat(loops // 2, loops // 4 * 3, gather_local)
        wait(hop)
        here = total.at[layer, pl.ds(core * (width // 2) + x * (width // 8), width // 8)]
        hop = [
            exchange(layer, k + 12, here, here, x_others[k - 1]) for k in range(1, NX)
        ]
        start(hop)
        repeat(loops // 4 * 3, loops, gather_local)
        wait(hop)
        here = total.at[layer, pl.ds(core * (width // 2), width // 2)]
        hop = [exchange(layer, 16, here, here, twin)]
        start(hop)
        wait(hop)
        summary = total[layer].astype(BF16)
        wo, wm = wo_ref[layer], wm_ref[layer]
        gain = gain_ref[pl.ds(layer, 1), :]

        def attend(i):
            rows = pl.ds(i * ROWS, ROWS)
            mixed = dot(query[rows, :], summary)
            scale = lax.rsqrt(jnp.mean(mixed * mixed, axis=-1, keepdims=True) + epsilon)
            attended = (mixed * scale * gain).astype(BF16)
            res[rows, :] = hidden(i).astype(F32) + dot(attended, wo)

        repeat(0, steps, attend)

        def arrived(k):
            for side in range(2):
                halo_copy(layer, side, k).wait()

        repeat(0, side_tiles, arrived)

        def out_copy(i):
            at = pl.ds(i * some_tiles, some_tiles)
            return pltpu.make_async_copy(hid.at[at], out_ref.at[at], out_sem.at[i])

        def finish(i):
            for u in range(some_tiles):
                t = i * some_tiles + u
                tiles_here = [halos[layer][far_ref[t * slots + j]] for j in range(slots)]
                rows = pl.ds(t * tile, tile)
                local[rows, :] += dot(blocks_of(t), jnp.concatenate(tiles_here, axis=0))
            rows = pl.ds(i * ROWS, ROWS)
            message = silu(dot(local[rows, :].astype(BF16), wm))
            new = jnp.where(keep(i), res[rows, :] + message, 0.0).astype(BF16)
            set_hidden(i, new)
            if layer < layers - 1:
                widen(i, new.astype(F32))
            else:
                out_copy(i).start()

        repeat(0, steps, finish)
        if layer == layers - 1:
            repeat(0, steps, lambda i: out_copy(i).wait())


def on_device(
    node_features,
    vertex_count,
    send_rows,
    block_values,
    block_cols,
    block_count,
    w_query,
    w_key,
    w_value,
    w_message,
    w_out,
    attn_gain,
):
    vertices, width = node_features.shape
    tiles, slots, tile, _ = block_values.shape
    layers = w_query.shape[0]
    halo_rows = send_rows.shape[2]
    side_tiles = halo_rows // tile
    steps = vertices // ROWS
    smem = pl.BlockSpec(memory_space=pltpu.SMEM)
    vmem = pl.BlockSpec(memory_space=pltpu.VMEM)
    anywhere = pl.BlockSpec(memory_space=pl.ANY)
    hops = 17

    part = lax.axis_index(("dom", "grp"))
    parts = lax.axis_size(("dom", "grp"))
    live = jnp.arange(slots, dtype=jnp.int32)[None, :] < block_count[:, None]
    near = jnp.where(live & (block_cols < tiles), block_cols, tiles)
    first = tiles + jnp.where(part > 0, 0, side_tiles)
    last = tiles + jnp.where(part < parts - 1, 2 * side_tiles, side_tiles)
    far = jnp.where(live & (block_cols >= first) & (block_cols < last), block_cols - tiles, 2 * side_tiles)
    out = pl.pallas_call(
        functools.partial(kernel, (layers, vertices, width, tile, slots, halo_rows)),
        out_shape=jax.ShapeDtypeStruct((tiles, tile, width), BF16),
        in_specs=[smem] * 4 + [anywhere] * 2 + [vmem] * 6,
        out_specs=anywhere,
        scratch_shapes=[
            pltpu.VMEM((tiles + 1, tile, width), BF16),
            pltpu.VMEM((2 * side_tiles + 1, tile, width), BF16),
            pltpu.VMEM((2 * side_tiles + 1, tile, width), BF16),
            pltpu.VMEM((2 * vertices, width // 2), F32),
            pltpu.VMEM((2, 2 * tile, width // 2), F32),
            pltpu.VMEM((2, side_tiles, tile, width), BF16),
            pltpu.VMEM((vertices, width), BF16),
            pltpu.VMEM((vertices, width), F32),
            pltpu.VMEM((vertices, width), F32),
            pltpu.VMEM((tiles, slots, tile, tile), BF16),
            pltpu.VMEM((width, width), F32),
            pltpu.VMEM((width // 2, width), F32),
            pltpu.VMEM((width // 8, width), F32),
            pltpu.VMEM((width // 32, width), F32),
            pltpu.VMEM((layers, width // 2, width), F32),
            pltpu.VMEM((layers, 3, width // 8, width), F32),
            pltpu.VMEM((layers, 3, width // 32, width), F32),
            pltpu.VMEM((layers, 3, width // 32, width), F32),
            pltpu.VMEM((layers, width, width), F32),
            pltpu.SemaphoreType.DMA((steps,)),
            pltpu.SemaphoreType.DMA((tiles,)),
            pltpu.SemaphoreType.DMA((steps,)),
            pltpu.SemaphoreType.DMA((2, side_tiles)),
            pltpu.SemaphoreType.DMA((layers, 2, side_tiles)),
            pltpu.SemaphoreType.DMA((layers, hops)),
            pltpu.SemaphoreType.DMA((layers, hops)),
        ],
        compiler_params=pltpu.CompilerParams(
            collective_id=0, has_side_effects=True, vmem_limit_bytes=67043328
        ),
        name="graph_layers",
    )(
        vertex_count,
        send_rows[0],
        near.reshape(-1),
        far.reshape(-1),
        node_features.reshape(tiles, tile, width),
        block_values,
        w_query,
        w_key,
        w_value,
        w_message,
        w_out,
        attn_gain,
    )
    return out.reshape(vertices, width)


def solution(mesh):
    placed = (
        P(("dom", "grp"), None),
        P(("dom", "grp")),
        P(("dom", "grp"), None, None),
        P(("dom", "grp"), None, None, None),
        P(("dom", "grp"), None),
        P(("dom", "grp")),
        P(),
        P(),
        P(),
        P(),
        P(),
        P(),
    )
    return jax.shard_map(
        on_device, mesh=mesh, in_specs=placed, out_specs=P(("dom", "grp"), None), check_vma=False
    )
```

time: 403 us -> 143 us (0.35); the launches traced: 396 us -> 143 us
  blocking collectives: 174 us -> 0 us
  Pallas kernels: 0 us -> 135 us
  matrix products: 105 us -> 0 us
  local copies, waits for them, and re-layouts: 59.9 us -> 5.99 us
  other arithmetic: 43.7 us -> 0.69 us
  starting transfers between devices: 12.5 us -> 0 us
    psum x2 -> x0, blocking collectives: 174 us -> none  [on_device(): summary_cast = lax.psum(partial_value, ('dom', 'grp')).astype(jnp.bfloat16)]
    pallas_call x0 -> x1, Pallas kernels: none -> 135 us  [on_device(): pl.pallas_call(functools.partial(kernel, (layers, vertices, width, tile,...]
    dot_general x12 -> x0, matrix products: 105 us -> none  [the longest x2 25.2 us: on_device(): jnp.einsum('tjab,tjbd->tad', used_blocks, picked, preferred_element_type=...]
    gather x4 -> x0, local copies, waits for them, and re-layouts: 57.2 us -> none  [the longest x2 31.5 us: on_device(): outgoing = hidden[send_rows[0]]]
    concatenate x2 -> x0, other arithmetic: 37.6 us -> none  [on_device(): extended = jnp.concatenate([hidden, lower_rows, upper_rows], axis=0)]
    ppermute x4 -> x0, starting transfers between devices: 12.5 us -> none  [the longest x2 8.67 us: extended_2(): lax.ppermute(lax.slice_in_dim(block, 0, width, axis=dim), axis, backward)]
    select_n x2 -> x1, other arithmetic: 5.24 us -> 0.69 us  [on_device(): jnp.where(live & (block_cols >= first) & (block_cols < last), block_cols...]
    unnamed x25 -> x1, local copies, waits for them, and re-layouts: 0.05 us -> 4.47 us
  transfers between devices with their start and end apart: 4 -> 0, of which waited for: 0 -> 0; matrix products, arithmetic and copies ran while one was open for 12% -> 0% of each run, Pallas kernels for 0% -> 0%
where the time goes in v1:
time: 143 us
  Pallas kernels  135 us (94%)
  local copies, waits for them, and re-layouts  5.99 us (4%)
    pallas_call x1, Pallas kernels, on_device(): pl.pallas_call(functools.partial(kernel, (layers, vertices, width, tile,...  135 us
    unnamed x1, local copies, waits for them, and re-layouts  4.47 us

profile of v1, /device:TPU:1, one launch (start us, length us, event | category | flops | bytes accessed | tf_op | source)
XLA Modules:
  0.0 142.5 jit_solution(18427036583255340593)
XLA Ops:
  0.7 0.7 add_select_fusion
  1.3 0.1 copy.14
  1.4 0.7 reshape.14.far_ref
  2.1 0.1 copy.13
  2.2 0.7 reshape.13.near_ref
  2.9 135.2 %graph_layers.1 = bf16[64,128,256]{2,1,0:T(8,128)(2,1)} custom-call(s32[1]{0:T(128)S(6)} %copy.16.count_ref, s32[2,2048]{1,0:T(2,128)} %bitcast.5, s32[256]{0:T(256)} %reshape.13.near_ref, s32[256]{0:T(256)} %reshape.14.far_ref, bf16[64,128,256]{2,1,0:T(8,128)(2,1)} %bitcast.4, bf16[64,4,128,128]{3,2,1,0:T(8,128)(2,1)} %blocks_ref.1, ...), custom_call_target="tpu_custom_call" | custom-call | tf_op jit(solution)/shard_map/graph_layers/pallas_call | solution.py:395
  138.1 4.5 %copy.17 = bf16[8192,256]{1,0:T(8,128)(2,1)} copy(bf16[8192,256]{1,0:T(8,128)(2,1)} %bitcast.3) | data formatting | bytes 8388608

commit v2 on v1

--- a/solution.py
+++ b/solution.py
@@ -14,7 +14,8 @@
 
 NX, NY, NZ = 4, 4, 4
 ROWS = 512
-UNROLL = 16
+UNROLL = 32
+BLOCK_COPIES = 4
 FIRST = 8
 
 
@@ -42,8 +43,8 @@
     sizes,
     count_ref,
     rows_ref,
-    near_ref,
-    far_ref,
+    cols_ref,
+    used_ref,
     feat_ref,
     blocks_ref,
     wq_ref,
@@ -72,9 +73,10 @@
     r3,
     r4,
     total,
+    near_ref,
+    far_ref,
     feat_sem,
     blk_sem,
-    out_sem,
     halo_send,
     halo_recv,
     ar_send,
@@ -124,7 +126,8 @@
         return pltpu.make_async_copy(feat_ref.at[at], hid.at[at], feat_sem.at[i])
 
     def blk_copy(i):
-        return pltpu.make_async_copy(blocks_ref.at[i], blk.at[i], blk_sem.at[i])
+        at = pl.ds(i * (tiles // BLOCK_COPIES), tiles // BLOCK_COPIES)
+        return pltpu.make_async_copy(blocks_ref.at[at], blk.at[at], blk_sem.at[i])
 
     for i in range(steps):
         feat_copy(i).start()
@@ -139,9 +142,12 @@
     for halo in halos:
         halo[2 * side_tiles] = jnp.zeros((tile, width), BF16)
 
-    def keep(i):
-        at = i * ROWS + lax.broadcasted_iota(jnp.int32, (ROWS, width), 0)
-        return at < count
+    def keep(i, new):
+        at = i * ROWS + lax.broadcasted_iota(jnp.int32, (ROWS, lanes), 0)
+        used = at < count
+        return jnp.concatenate(
+            [jnp.where(used, new[:, :lanes], 0.0), jnp.where(used, new[:, lanes:], 0.0)], axis=1
+        )
 
     def widen(i, new):
         wide[pl.ds(2 * i * ROWS, ROWS, stride=2), :] = new[:, :lanes]
@@ -149,12 +155,13 @@
 
     def enter(i):
         feat_copy(i).wait()
-        kept = jnp.where(keep(i), hidden(i).astype(F32), 0.0)
+        kept = keep(i, hidden(i).astype(F32))
         set_hidden(i, kept.astype(BF16))
         widen(i, kept)
 
     repeat(0, steps, enter)
-    repeat(0, tiles, lambda i: blk_copy(i).start())
+    for i in range(BLOCK_COPIES):
+        blk_copy(i).start()
     pl.semaphore_wait(barrier, len(partners))
 
     def halo_copy(layer, side, k):
@@ -171,11 +178,14 @@
     def gather(layer, first, last):
         def chunk(k):
             for side in range(2):
+                base = (2 * k + side) * tile
+
                 def some(i):
+                    at = i * UNROLL
+                    some_rows = [rows_ref[base + at + u] for u in range(UNROLL)]
+                    loaded = [wide[pl.ds(2 * row, 2), :] for row in some_rows]
                     for u in range(UNROLL):
-                        at = i * UNROLL + u
-                        row = rows_ref[side, k * tile + at]
-                        picked[side, pl.ds(2 * at, 2), :] = wide[pl.ds(2 * row, 2), :]
+                        picked[side, pl.ds(2 * (at + u), 2), :] = loaded[u]
 
                 repeat(0, tile // UNROLL, some)
                 send[side, k, :, :lanes] = picked[side, pl.ds(0, tile, stride=2), :].astype(BF16)
@@ -184,6 +194,21 @@
                 halo_copy(layer, side, k).start()
 
         repeat(first, last, chunk)
+
+    def between(value, low, high):
+        return jnp.minimum(jnp.maximum(value, low), high)
+
+    first = tiles + side_tiles * between(1 - part, 0, 1)
+    last = tiles + side_tiles * (1 + between(parts - 1 - part, 0, 1))
+
+    def index(t):
+        for j in range(slots):
+            col = cols_ref[j, t]
+            live = between(used_ref[t] - j, 0, 1)
+            own = live * between(tiles - col, 0, 1)
+            near_ref[t * slots + j] = tiles + (col - tiles) * own
+            side = live * between(col - first + 1, 0, 1) * between(last - col, 0, 1)
+            far_ref[t * slots + j] = 2 * side_tiles + (col - tiles - 2 * side_tiles) * side
 
     def exchange(layer, number, src, dst, target):
         return pltpu.make_async_remote_copy(
@@ -212,6 +237,8 @@
 
         gather(layer, 0, FIRST)
 
+        if layer == 0:
+            repeat(0, tiles, index)
         summ[...] = jnp.zeros_like(summ)
 
         def add_summary(i):
@@ -232,14 +259,15 @@
         def gather_local(i):
             for u in range(group):
                 t = i * group + u
-                if layer == 0:
-                    blk_copy(t).wait()
                 tiles_here = [hid[near_ref[t * slots + j]] for j in range(slots)]
                 local[pl.ds(t * tile, tile), :] = dot(
                     blocks_of(t), jnp.concatenate(tiles_here, axis=0)
                 )
 
         loops = tiles // group
+        if layer == 0:
+            for i in range(BLOCK_COPIES):
+                blk_copy(i).wait()
 
         share = width // 2
         hop = [
@@ -336,28 +364,24 @@
 
         repeat(0, side_tiles, arrived)
 
-        def out_copy(i):
-            at = pl.ds(i * some_tiles, some_tiles)
-            return pltpu.make_async_copy(hid.at[at], out_ref.at[at], out_sem.at[i])
-
         def finish(i):
+            parts_here = []
             for u in range(some_tiles):
                 t = i * some_tiles + u
                 tiles_here = [halos[layer][far_ref[t * slots + j]] for j in range(slots)]
-                rows = pl.ds(t * tile, tile)
-                local[rows, :] += dot(blocks_of(t), jnp.concatenate(tiles_here, axis=0))
-            rows = pl.ds(i * ROWS, ROWS)
-            message = silu(dot(local[rows, :].astype(BF16), wm))
-            new = jnp.where(keep(i), res[rows, :] + message, 0.0).astype(BF16)
-            set_hidden(i, new)
+                both = local[pl.ds(t * tile, tile), :] + dot(
+                    blocks_of(t), jnp.concatenate(tiles_here, axis=0)
+                )
+                parts_here.append(both.astype(BF16))
+            message = silu(dot(jnp.concatenate(parts_here, axis=0), wm))
+            new = keep(i, res[pl.ds(i * ROWS, ROWS), :] + message).astype(BF16)
             if layer < layers - 1:
+                set_hidden(i, new)
                 widen(i, new.astype(F32))
             else:
-                out_copy(i).start()
+                out_ref[pl.ds(i * some_tiles, some_tiles)] = new.reshape(some_tiles, tile, width)
 
         repeat(0, steps, finish)
-        if layer == layers - 1:
-            repeat(0, steps, lambda i: out_copy(i).wait())
 
 
 def on_device(
@@ -385,18 +409,11 @@
     anywhere = pl.BlockSpec(memory_space=pl.ANY)
     hops = 17
 
-    part = lax.axis_index(("dom", "grp"))
-    parts = lax.axis_size(("dom", "grp"))
-    live = jnp.arange(slots, dtype=jnp.int32)[None, :] < block_count[:, None]
-    near = jnp.where(live & (block_cols < tiles), block_cols, tiles)
-    first = tiles + jnp.where(part > 0, 0, side_tiles)
-    last = tiles + jnp.where(part < parts - 1, 2 * side_tiles, side_tiles)
-    far = jnp.where(live & (block_cols >= first) & (block_cols < last), block_cols - tiles, 2 * side_tiles)
     out = pl.pallas_call(
         functools.partial(kernel, (layers, vertices, width, tile, slots, halo_rows)),
-        out_shape=jax.ShapeDtypeStruct((tiles, tile, width), BF16),
+        out_shape=pltpu.VMEM((tiles, tile, width), BF16),
         in_specs=[smem] * 4 + [anywhere] * 2 + [vmem] * 6,
-        out_specs=anywhere,
+        out_specs=vmem,
         scratch_shapes=[
             pltpu.VMEM((tiles + 1, tile, width), BF16),
             pltpu.VMEM((2 * side_tiles + 1, tile, width), BF16),
@@ -417,23 +434,24 @@
             pltpu.VMEM((layers, 3, width // 32, width), F32),
             pltpu.VMEM((layers, 3, width // 32, width), F32),
             pltpu.VMEM((layers, width, width), F32),
+            pltpu.SMEM((tiles * slots,), jnp.int32),
+            pltpu.SMEM((tiles * slots,), jnp.int32),
             pltpu.SemaphoreType.DMA((steps,)),
-            pltpu.SemaphoreType.DMA((tiles,)),
-            pltpu.SemaphoreType.DMA((steps,)),
+            pltpu.SemaphoreType.DMA((BLOCK_COPIES,)),
             pltpu.SemaphoreType.DMA((2, side_tiles)),
             pltpu.SemaphoreType.DMA((layers, 2, side_tiles)),
             pltpu.SemaphoreType.DMA((layers, hops)),
             pltpu.SemaphoreType.DMA((layers, hops)),
         ],
         compiler_params=pltpu.CompilerParams(
-            collective_id=0, has_side_effects=True, vmem_limit_bytes=67043328
+            collective_id=0, has_side_effects=True, vmem_limit_bytes=58 * 2**20
         ),
         name="graph_layers",
     )(
         vertex_count,
-        send_rows[0],
-        near.reshape(-1),
-        far.reshape(-1),
+        send_rows[0].reshape(2, side_tiles, tile).transpose(1, 0, 2).reshape(-1),
+        block_cols.T,
+        block_count,
         node_features.reshape(tiles, tile, width),
         block_values,
         w_query,

time: 143 us -> 129 us (0.902)
  Pallas kernels: 135 us -> 126 us
  local copies, waits for them, and re-layouts: 5.99 us -> 2.02 us
    pallas_call x1, Pallas kernels: 135 us -> 126 us  [on_device(): pl.pallas_call(functools.partial(kernel, (layers, vertices, width, tile,...]
    unnamed x1, local copies, waits for them, and re-layouts: 4.47 us -> 2.02 us
where the time goes in v2:
time: 129 us
  Pallas kernels  126 us (98%)
  local copies, waits for them, and re-layouts  2.02 us (2%)
    pallas_call x1, Pallas kernels, on_device(): pl.pallas_call(functools.partial(kernel, (layers, vertices, width, tile,...  126 us

profile of v2, /device:TPU:1, one launch (start us, length us, event | category | flops | bytes accessed | tf_op | source)
XLA Modules:
  0.0 129.0 jit_solution(6545175511286851608)
XLA Ops:
  0.7 126.4 %graph_layers.1 = bf16[64,128,256]{2,1,0:T(8,128)(2,1)S(1)} custom-call(s32[1]{0:T(128)S(6)} %copy.16.count_ref, s32[4096]{0:T(1024)} %bitcast.10, s32[4,64]{1,0:T(4,128)} %bitcast.11, s32[64]{0:T(128)} %used_ref.1, bf16[64,128,256]{2,1,0:T(8,128)(2,1)} %bitcast.9, bf16[64,4,128,128]{3,2,1,0:T(8,128)(2,1)} %blocks_ref.1, bf16[2,256,256]{2,1,0:T(8,128)(2,1)} %wq_ref.1, ...), custom_call_target="tpu_custom_call" | custom-call | tf_op jit(solution)/shard_map/graph_layers/pallas_call | solution.py:412
  127.0 2.0 %copy.15 = bf16[8192,256]{1,0:T(8,128)(2,1)} copy(bf16[8192,256]{1,0:T(8,128)(2,1)S(1)} %bitcast.8) | data formatting | bytes 8388608

commit v3 on v2

--- a/solution.py
+++ b/solution.py
@@ -13,7 +13,9 @@
 BF16 = jnp.bfloat16
 
 NX, NY, NZ = 4, 4, 4
-ROWS = 512
+ROWS = 4096
+ENTRY_ROWS = 1024
+GROUP = 16
 UNROLL = 32
 BLOCK_COPIES = 4
 FIRST = 8
@@ -121,15 +123,18 @@
     def set_hidden(i, new):
         hid[pl.ds(i * some_tiles, some_tiles)] = new.reshape(some_tiles, tile, width)
 
+    entry_tiles = ENTRY_ROWS // tile
+    entries = vertices // ENTRY_ROWS
+
     def feat_copy(i):
-        at = pl.ds(i * some_tiles, some_tiles)
+        at = pl.ds(i * entry_tiles, entry_tiles)
         return pltpu.make_async_copy(feat_ref.at[at], hid.at[at], feat_sem.at[i])
 
     def blk_copy(i):
         at = pl.ds(i * (tiles // BLOCK_COPIES), tiles // BLOCK_COPIES)
         return pltpu.make_async_copy(blocks_ref.at[at], blk.at[at], blk_sem.at[i])
 
-    for i in range(steps):
+    for i in range(entries):
         feat_copy(i).start()
 
     barrier = pltpu.get_barrier_semaphore()
@@ -142,24 +147,25 @@
     for halo in halos:
         halo[2 * side_tiles] = jnp.zeros((tile, width), BF16)
 
-    def keep(i, new):
-        at = i * ROWS + lax.broadcasted_iota(jnp.int32, (ROWS, lanes), 0)
+    def keep(first, new):
+        at = first + lax.broadcasted_iota(jnp.int32, (new.shape[0], lanes), 0)
         used = at < count
         return jnp.concatenate(
             [jnp.where(used, new[:, :lanes], 0.0), jnp.where(used, new[:, lanes:], 0.0)], axis=1
         )
 
-    def widen(i, new):
-        wide[pl.ds(2 * i * ROWS, ROWS, stride=2), :] = new[:, :lanes]
-        wide[pl.ds(2 * i * ROWS + 1, ROWS, stride=2), :] = new[:, lanes:]
+    def widen(first, new):
+        wide[pl.ds(2 * first, new.shape[0], stride=2), :] = new[:, :lanes]
+        wide[pl.ds(2 * first + 1, new.shape[0], stride=2), :] = new[:, lanes:]
 
     def enter(i):
         feat_copy(i).wait()
-        kept = keep(i, hidden(i).astype(F32))
-        set_hidden(i, kept.astype(BF16))
-        widen(i, kept)
-
-    repeat(0, steps, enter)
+        at = pl.ds(i * entry_tiles, entry_tiles)
+        kept = keep(i * ENTRY_ROWS, hid[at].reshape(ENTRY_ROWS, width).astype(F32))
+        hid[at] = kept.astype(BF16).reshape(entry_tiles, tile, width)
+        widen(i * ENTRY_ROWS, kept)
+
+    repeat(0, entries, enter)
     for i in range(BLOCK_COPIES):
         blk_copy(i).start()
     pl.semaphore_wait(barrier, len(partners))
@@ -254,17 +260,16 @@
             rows = pl.ds(i * ROWS, ROWS)
             query[rows, :] = feature_map(dot(hidden(i), wq)).astype(BF16)
 
-        group = 4
 
         def gather_local(i):
-            for u in range(group):
-                t = i * group + u
+            for u in range(GROUP):
+                t = i * GROUP + u
                 tiles_here = [hid[near_ref[t * slots + j]] for j in range(slots)]
                 local[pl.ds(t * tile, tile), :] = dot(
                     blocks_of(t), jnp.concatenate(tiles_here, axis=0)
                 )
 
-        loops = tiles // group
+        loops = tiles // GROUP
         if layer == 0:
             for i in range(BLOCK_COPIES):
                 blk_copy(i).wait()
@@ -374,10 +379,10 @@
                 )
                 parts_here.append(both.astype(BF16))
             message = silu(dot(jnp.concatenate(parts_here, axis=0), wm))
-            new = keep(i, res[pl.ds(i * ROWS, ROWS), :] + message).astype(BF16)
+            new = keep(i * ROWS, res[pl.ds(i * ROWS, ROWS), :] + message).astype(BF16)
             if layer < layers - 1:
                 set_hidden(i, new)
-                widen(i, new.astype(F32))
+                widen(i * ROWS, new.astype(F32))
             else:
                 out_ref[pl.ds(i * some_tiles, some_tiles)] = new.reshape(some_tiles, tile, width)
 
@@ -403,7 +408,6 @@
     layers = w_query.shape[0]
     halo_rows = send_rows.shape[2]
     side_tiles = halo_rows // tile
-    steps = vertices // ROWS
     smem = pl.BlockSpec(memory_space=pltpu.SMEM)
     vmem = pl.BlockSpec(memory_space=pltpu.VMEM)
     anywhere = pl.BlockSpec(memory_space=pl.ANY)
@@ -436,7 +440,7 @@
             pltpu.VMEM((layers, width, width), F32),
             pltpu.SMEM((tiles * slots,), jnp.int32),
             pltpu.SMEM((tiles * slots,), jnp.int32),
-            pltpu.SemaphoreType.DMA((steps,)),
+            pltpu.SemaphoreType.DMA((vertices // ENTRY_ROWS,)),
             pltpu.SemaphoreType.DMA((BLOCK_COPIES,)),
             pltpu.SemaphoreType.DMA((2, side_tiles)),
             pltpu.SemaphoreType.DMA((layers, 2, side_tiles)),

time: 129 us -> 123 us (0.953)
  Pallas kernels: 126 us -> 120 us
    pallas_call x1, Pallas kernels: 126 us -> 120 us  [on_device(): pl.pallas_call(functools.partial(kernel, (layers, vertices, width, tile,...]
where the time goes in v3:
time: 123 us; the launch traced here: 122 us
  Pallas kernels  120 us (98%)
  local copies, waits for them, and re-layouts  2.02 us (2%)
    pallas_call x1, Pallas kernels, on_device(): pl.pallas_call(functools.partial(kernel, (layers, vertices, width, tile,...  120 us

profile of v3, /device:TPU:1, one launch (start us, length us, event | category | flops | bytes accessed | tf_op | source)
XLA Modules:
  0.0 122.4 jit_solution(15071425237733898893)
XLA Ops:
  0.7 119.8 %graph_layers.1 = bf16[64,128,256]{2,1,0:T(8,128)(2,1)S(1)} custom-call(s32[1]{0:T(128)S(6)} %copy.16.count_ref, s32[4096]{0:T(1024)} %bitcast.10, s32[4,64]{1,0:T(4,128)} %bitcast.11, s32[64]{0:T(128)} %used_ref.1, bf16[64,128,256]{2,1,0:T(8,128)(2,1)} %bitcast.9, bf16[64,4,128,128]{3,2,1,0:T(8,128)(2,1)} %blocks_ref.1, bf16[2,256,256]{2,1,0:T(8,128)(2,1)} %wq_ref.1, ...), custom_call_target="tpu_custom_call" | custom-call | tf_op jit(solution)/shard_map/graph_layers/pallas_call | solution.py:416
  120.4 2.0 %copy.15 = bf16[8192,256]{1,0:T(8,128)(2,1)} copy(bf16[8192,256]{1,0:T(8,128)(2,1)S(1)} %bitcast.8) | data formatting | bytes 8388608

commit v4 on v3

--- a/solution.py
+++ b/solution.py
@@ -15,10 +15,13 @@
 NX, NY, NZ = 4, 4, 4
 ROWS = 4096
 ENTRY_ROWS = 1024
+FINISH = 512
 GROUP = 16
 UNROLL = 32
 BLOCK_COPIES = 4
-FIRST = 8
+CHUNK = 2
+FIRST = 1
+SECOND = 3
 
 
 def repeat(start, stop, body):
@@ -34,7 +37,8 @@
 
 
 def silu(u):
-    return 0.5 * u * (1.0 + jnp.tanh(0.5 * u))
+    h = 0.5 * u
+    return h + h * jnp.tanh(h)
 
 
 def dot(a, b):
@@ -49,13 +53,19 @@
     used_ref,
     feat_ref,
     blocks_ref,
+    wq_hbm,
+    wk_hbm,
+    wv_hbm,
+    wm_hbm,
+    wo_hbm,
+    gain_hbm,
+    out_ref,
     wq_ref,
     wk_ref,
     wv_ref,
     wm_ref,
     wo_ref,
     gain_ref,
-    out_ref,
     hid,
     halo_0,
     halo_1,
@@ -77,6 +87,7 @@
     total,
     near_ref,
     far_ref,
+    weight_sem,
     feat_sem,
     blk_sem,
     halo_send,
@@ -134,8 +145,23 @@
         at = pl.ds(i * (tiles // BLOCK_COPIES), tiles // BLOCK_COPIES)
         return pltpu.make_async_copy(blocks_ref.at[at], blk.at[at], blk_sem.at[i])
 
+    weight_copies = [
+        pltpu.make_async_copy(src, dst, weight_sem.at[i])
+        for i, (src, dst) in enumerate(
+            (
+                (wk_hbm, wk_ref),
+                (wv_hbm, wv_ref),
+                (wq_hbm, wq_ref),
+                (wm_hbm, wm_ref),
+                (wo_hbm, wo_ref),
+                (gain_hbm, gain_ref),
+            )
+        )
+    ]
     for i in range(entries):
         feat_copy(i).start()
+    for copy in weight_copies:
+        copy.start()
 
     barrier = pltpu.get_barrier_semaphore()
     partners = [upper, lower, twin] + x_others + y_others + z_others
@@ -173,8 +199,8 @@
     def halo_copy(layer, side, k):
         at = (1 - side) * side_tiles
         return pltpu.make_async_remote_copy(
-            src_ref=send.at[side, k],
-            dst_ref=halos[layer].at[at + k],
+            src_ref=send.at[side, pl.ds(k * CHUNK, CHUNK)],
+            dst_ref=halos[layer].at[pl.ds(at + k * CHUNK, CHUNK)],
             send_sem=halo_send.at[side, k],
             recv_sem=halo_recv.at[layer, side, k],
             device_id=lower if side == 0 else upper,
@@ -182,20 +208,26 @@
         )
 
     def gather(layer, first, last):
+        def one_tile(side, k):
+            base = (2 * k + side) * tile
+
+            def some(i):
+                at = i * UNROLL
+                some_rows = [rows_ref[base + at + u] for u in range(UNROLL)]
+                loaded = [wide[pl.ds(2 * row, 2), :] for row in some_rows]
+                for u in range(UNROLL):
+                    picked[side, pl.ds(2 * (at + u), 2), :] = loaded[u]
+
+            repeat(0, tile // UNROLL, some)
+            send[side, k, :, :lanes] = picked[side, pl.ds(0, tile, stride=2), :].astype(BF16)
+            send[side, k, :, lanes:] = picked[side, pl.ds(1, tile, stride=2), :].astype(BF16)
+
         def chunk(k):
             for side in range(2):
-                base = (2 * k + side) * tile
-
-                def some(i):
-                    at = i * UNROLL
-                    some_rows = [rows_ref[base + at + u] for u in range(UNROLL)]
-                    loaded = [wide[pl.ds(2 * row, 2), :] for row in some_rows]
-                    for u in range(UNROLL):
-                        picked[side, pl.ds(2 * (at + u), 2), :] = loaded[u]
-
-                repeat(0, tile // UNROLL, some)
-                send[side, k, :, :lanes] = picked[side, pl.ds(0, tile, stride=2), :].astype(BF16)
-                send[side, k, :, lanes:] = picked[side, pl.ds(1, tile, stride=2), :].astype(BF16)
+                if CHUNK == 1:
+                    one_tile(side, k)
+                else:
+                    repeat(k * CHUNK, (k + 1) * CHUNK, lambda t: one_tile(side, t))
             for side in range(2):
                 halo_copy(layer, side, k).start()
 
@@ -238,13 +270,12 @@
         return jnp.concatenate([blk[t, j] for j in range(slots)], axis=1)
 
     for layer in range(layers):
+        gather(layer, 0, FIRST)
+        if layer == 0:
+            for copy in weight_copies:
+                copy.wait()
         wk_t = wk_ref[layer].T
         wv, wq = wv_ref[layer], wq_ref[layer]
-
-        gather(layer, 0, FIRST)
-
-        if layer == 0:
-            repeat(0, tiles, index)
         summ[...] = jnp.zeros_like(summ)
 
         def add_summary(i):
@@ -270,16 +301,18 @@
                 )
 
         loops = tiles // GROUP
-        if layer == 0:
-            for i in range(BLOCK_COPIES):
-                blk_copy(i).wait()
+
+        gather(layer, FIRST, SECOND)
 
         share = width // 2
         hop = [
             exchange(layer, 0, summ.at[pl.ds((1 - core) * share, share)], r1.at[layer], twin)
         ]
         start(hop)
-        repeat(0, steps // 2, ask)
+        if layer == 0:
+            repeat(0, tiles, index)
+        else:
+            repeat(0, steps // 2, ask)
         wait(hop)
         half[...] = summ[pl.ds(core * share, share), :] + r1[layer]
 
@@ -295,60 +328,48 @@
             for k in range(1, NX)
         ]
         start(hop)
-        repeat(steps // 2, steps, ask)
+        repeat(0 if layer == 0 else steps // 2, steps, ask)
         wait(hop)
         quarter[...] = half[pl.ds(x * share, share), :] + (
             r2[layer, 0] + r2[layer, 1] + r2[layer, 2]
         )
 
-        share //= NY
         hop = [
-            exchange(
-                layer,
-                k + 3,
-                quarter.at[pl.ds(lax.rem(y + k, NY) * share, share)],
-                r3.at[layer, k - 1],
-                y_others[k - 1],
-            )
+            exchange(layer, k + 3, quarter, r3.at[layer, k - 1], y_others[k - 1])
             for k in range(1, NY)
         ]
         start(hop)
+        if layer == 0:
+            for i in range(BLOCK_COPIES):
+                blk_copy(i).wait()
         repeat(0, loops // 4, gather_local)
         wait(hop)
-        piece[...] = quarter[pl.ds(y * share, share), :] + (
-            r3[layer, 0] + r3[layer, 1] + r3[layer, 2]
-        )
+        piece[...] = quarter[...] + (r3[layer, 0] + r3[layer, 1] + r3[layer, 2])
 
         hop = [
             exchange(layer, k + 6, piece, r4.at[layer, k - 1], z_others[k - 1])
             for k in range(1, NZ)
         ]
         start(hop)
-        gather(layer, FIRST, side_tiles)
+        gather(layer, SECOND, side_tiles // CHUNK)
         repeat(loops // 4, loops // 2, gather_local)
         wait(hop)
-        at = core * (width // 2) + x * (width // 8) + y * share
+        at = core * (width // 2) + x * share
         total[layer, pl.ds(at, share), :] = piece[...] + (
             r4[layer, 0] + r4[layer, 1] + r4[layer, 2]
         )
 
         here = total.at[layer, pl.ds(at, share)]
         hop = [
-            exchange(layer, k + 9, here, here, y_others[k - 1]) for k in range(1, NY)
+            exchange(layer, k + 9, here, here, x_others[k - 1]) for k in range(1, NX)
         ]
         start(hop)
         repeat(loops // 2, loops // 4 * 3, gather_local)
         wait(hop)
-        here = total.at[layer, pl.ds(core * (width // 2) + x * (width // 8), width // 8)]
-        hop = [
-            exchange(layer, k + 12, here, here, x_others[k - 1]) for k in range(1, NX)
-        ]
+        here = total.at[layer, pl.ds(core * (width // 2), width // 2)]
+        hop = [exchange(layer, 13, here, here, twin)]
         start(hop)
         repeat(loops // 4 * 3, loops, gather_local)
-        wait(hop)
-        here = total.at[layer, pl.ds(core * (width // 2), width // 2)]
-        hop = [exchange(layer, 16, here, here, twin)]
-        start(hop)
         wait(hop)
         summary = total[layer].astype(BF16)
         wo, wm = wo_ref[layer], wm_ref[layer]
@@ -367,24 +388,30 @@
             for side in range(2):
                 halo_copy(layer, side, k).wait()
 
-        repeat(0, side_tiles, arrived)
-
-        def finish(i):
+        repeat(0, side_tiles // CHUNK, arrived)
+
+        def finish_some(first):
             parts_here = []
-            for u in range(some_tiles):
-                t = i * some_tiles + u
+            for u in range(FINISH // tile):
+                t = first * (FINISH // tile) + u
                 tiles_here = [halos[layer][far_ref[t * slots + j]] for j in range(slots)]
                 both = local[pl.ds(t * tile, tile), :] + dot(
                     blocks_of(t), jnp.concatenate(tiles_here, axis=0)
                 )
                 parts_here.append(both.astype(BF16))
             message = silu(dot(jnp.concatenate(parts_here, axis=0), wm))
-            new = keep(i * ROWS, res[pl.ds(i * ROWS, ROWS), :] + message).astype(BF16)
+            rows = first * FINISH
+            new = keep(rows, res[pl.ds(rows, FINISH), :] + message).astype(BF16)
+            at = pl.ds(first * (FINISH // tile), FINISH // tile)
             if layer < layers - 1:
-                set_hidden(i, new)
-                widen(i * ROWS, new.astype(F32))
+                hid[at] = new.reshape(FINISH // tile, tile, width)
+                widen(rows, new.astype(F32))
             else:
-                out_ref[pl.ds(i * some_tiles, some_tiles)] = new.reshape(some_tiles, tile, width)
+                out_ref[at] = new.reshape(FINISH // tile, tile, width)
+
+        def finish(i):
+            for k in range(ROWS // FINISH):
+                finish_some(i * (ROWS // FINISH) + k)
 
         repeat(0, steps, finish)
 
@@ -411,14 +438,16 @@
     smem = pl.BlockSpec(memory_space=pltpu.SMEM)
     vmem = pl.BlockSpec(memory_space=pltpu.VMEM)
     anywhere = pl.BlockSpec(memory_space=pl.ANY)
-    hops = 17
+    hops = 14
 
     out = pl.pallas_call(
         functools.partial(kernel, (layers, vertices, width, tile, slots, halo_rows)),
         out_shape=pltpu.VMEM((tiles, tile, width), BF16),
-        in_specs=[smem] * 4 + [anywhere] * 2 + [vmem] * 6,
+        in_specs=[smem] * 4 + [anywhere] * 8,
         out_specs=vmem,
-        scratch_shapes=[
+        scratch_shapes=[pltpu.VMEM((layers, width, width), BF16)] * 5
+        + [
+            pltpu.VMEM((layers, width), F32),
             pltpu.VMEM((tiles + 1, tile, width), BF16),
             pltpu.VMEM((2 * side_tiles + 1, tile, width), BF16),
             pltpu.VMEM((2 * side_tiles + 1, tile, width), BF16),
@@ -432,18 +461,19 @@
             pltpu.VMEM((width, width), F32),
             pltpu.VMEM((width // 2, width), F32),
             pltpu.VMEM((width // 8, width), F32),
-            pltpu.VMEM((width // 32, width), F32),
+            pltpu.VMEM((width // 8, width), F32),
             pltpu.VMEM((layers, width // 2, width), F32),
             pltpu.VMEM((layers, 3, width // 8, width), F32),
-            pltpu.VMEM((layers, 3, width // 32, width), F32),
-            pltpu.VMEM((layers, 3, width // 32, width), F32),
+            pltpu.VMEM((layers, 3, width // 8, width), F32),
+            pltpu.VMEM((layers, 3, width // 8, width), F32),
             pltpu.VMEM((layers, width, width), F32),
             pltpu.SMEM((tiles * slots,), jnp.int32),
             pltpu.SMEM((tiles * slots,), jnp.int32),
+            pltpu.SemaphoreType.DMA((6,)),
             pltpu.SemaphoreType.DMA((vertices // ENTRY_ROWS,)),
             pltpu.SemaphoreType.DMA((BLOCK_COPIES,)),
-            pltpu.SemaphoreType.DMA((2, side_tiles)),
-            pltpu.SemaphoreType.DMA((layers, 2, side_tiles)),
+            pltpu.SemaphoreType.DMA((2, side_tiles // CHUNK)),
+            pltpu.SemaphoreType.DMA((layers, 2, side_tiles // CHUNK)),
             pltpu.SemaphoreType.DMA((layers, hops)),
             pltpu.SemaphoreType.DMA((layers, hops)),
         ],

time: 123 us -> 115 us (0.935)
  Pallas kernels: 120 us -> 112 us
    pallas_call x1, Pallas kernels: 120 us -> 112 us  [on_device(): pl.pallas_call(functools.partial(kernel, (layers, vertices, width, tile,...]
where the time goes in v4:
time: 115 us
  Pallas kernels  112 us (97%)
  local copies, waits for them, and re-layouts  2.02 us (2%)
    pallas_call x1, Pallas kernels, on_device(): pl.pallas_call(functools.partial(kernel, (layers, vertices, width, tile,...  112 us

profile of v4, /device:TPU:1, one launch (start us, length us, event | category | flops | bytes accessed | tf_op | source)
XLA Modules:
  0.0 115.1 jit_solution(15317903919768539125)
XLA Ops:
  0.7 112.4 %graph_layers.1 = bf16[64,128,256]{2,1,0:T(8,128)(2,1)S(1)} custom-call(s32[1]{0:T(128)S(6)} %copy.16.count_ref, s32[4096]{0:T(1024)} %bitcast.10, s32[4,64]{1,0:T(4,128)} %bitcast.11, s32[64]{0:T(128)} %used_ref.1, bf16[64,128,256]{2,1,0:T(8,128)(2,1)} %bitcast.9, bf16[64,4,128,128]{3,2,1,0:T(8,128)(2,1)} %blocks_ref.1, bf16[2,256,256]{2,1,0:T(8,128)(2,1)} %wq_hbm.1, ...), custom_call_target="tpu_custom_call" | custom-call | tf_op jit(solution)/shard_map/graph_layers/pallas_call | solution.py:443
  113.0 2.0 %copy.15 = bf16[8192,256]{1,0:T(8,128)(2,1)} copy(bf16[8192,256]{1,0:T(8,128)(2,1)S(1)} %bitcast.8) | data formatting | bytes 8388608

commit v5 on v4

--- a/solution.py
+++ b/solution.py
@@ -15,13 +15,14 @@
 NX, NY, NZ = 4, 4, 4
 ROWS = 4096
 ENTRY_ROWS = 1024
-FINISH = 512
+FINISH = 1024
 GROUP = 16
 UNROLL = 32
 BLOCK_COPIES = 4
-CHUNK = 2
-FIRST = 1
-SECOND = 3
+CHUNKS = (1, 1, 2, 2, 2, 4, 4)
+FIRST = 2
+SECOND = 4
+THIRD = 5
 
 
 def repeat(start, stop, body):
@@ -36,8 +37,7 @@
     return jnp.maximum(u, 0.0) + jnp.exp(jnp.minimum(u, 0.0))
 
 
-def silu(u):
-    h = 0.5 * u
+def silu_of_twice(h):
     return h + h * jnp.tanh(h)
 
 
@@ -47,10 +47,10 @@
 
 def kernel(
     sizes,
-    count_ref,
-    rows_ref,
-    cols_ref,
-    used_ref,
+    count_hbm,
+    rows_hbm,
+    cols_hbm,
+    used_hbm,
     feat_ref,
     blocks_ref,
     wq_hbm,
@@ -67,6 +67,7 @@
     wo_ref,
     gain_ref,
     hid,
+    lifted,
     halo_0,
     halo_1,
     wide,
@@ -84,9 +85,16 @@
     r2,
     r3,
     r4,
+    r5,
+    coarse,
     total,
+    count_ref,
+    rows_ref,
+    cols_ref,
+    used_ref,
     near_ref,
     far_ref,
+    small_sem,
     weight_sem,
     feat_sem,
     blk_sem,
@@ -124,7 +132,8 @@
     twin = place(x, y, z, 1 - core)
     x_others = [place(lax.rem(x + k, NX), y, z, core) for k in range(1, NX)]
     y_others = [place(x, lax.rem(y + k, NY), z, core) for k in range(1, NY)]
-    z_others = [place(x, y, lax.rem(z + k, NZ), core) for k in range(1, NZ)]
+    z_far = place(x, y, NZ - 1 - z, core)
+    z_near = {"dom": dom, "grp": 1 - grp}
 
     some_tiles = ROWS // tile
 
@@ -160,16 +169,28 @@
     ]
     for i in range(entries):
         feat_copy(i).start()
-    for copy in weight_copies:
+    small_copies = [
+        pltpu.make_async_copy(src, dst, small_sem.at[i])
+        for i, (src, dst) in enumerate(
+            (
+                (count_hbm, count_ref),
+                (rows_hbm, rows_ref),
+                (cols_hbm, cols_ref),
+                (used_hbm, used_ref),
+            )
+        )
+    ]
+    for copy in small_copies + weight_copies:
         copy.start()
 
     barrier = pltpu.get_barrier_semaphore()
-    partners = [upper, lower, twin] + x_others + y_others + z_others
+    partners = [upper, lower, twin, z_far, z_near] + x_others + y_others
     for partner in partners:
         pl.semaphore_signal(barrier, inc=1, device_id=partner, device_id_type=MESH)
 
+    small_copies[0].wait()
     count = count_ref[0]
-    hid[tiles] = jnp.zeros((tile, width), BF16)
+    lifted[tiles] = jnp.zeros((tile, width), BF16)
     for halo in halos:
         halo[2 * side_tiles] = jnp.zeros((tile, width), BF16)
 
@@ -194,13 +215,15 @@
     repeat(0, entries, enter)
     for i in range(BLOCK_COPIES):
         blk_copy(i).start()
+    for copy in small_copies[1:]:
+        copy.wait()
     pl.semaphore_wait(barrier, len(partners))
 
     def halo_copy(layer, side, k):
-        at = (1 - side) * side_tiles
+        at = (1 - side) * side_tiles + sum(CHUNKS[:k])
         return pltpu.make_async_remote_copy(
-            src_ref=send.at[side, pl.ds(k * CHUNK, CHUNK)],
-            dst_ref=halos[layer].at[pl.ds(at + k * CHUNK, CHUNK)],
+            src_ref=send.at[side, pl.ds(sum(CHUNKS[:k]), CHUNKS[k])],
+            dst_ref=halos[layer].at[pl.ds(at, CHUNKS[k])],
             send_sem=halo_send.at[side, k],
             recv_sem=halo_recv.at[layer, side, k],
             device_id=lower if side == 0 else upper,
@@ -208,30 +231,25 @@
         )
 
     def gather(layer, first, last):
-        def one_tile(side, k):
-            base = (2 * k + side) * tile
-
-            def some(i):
-                at = i * UNROLL
-                some_rows = [rows_ref[base + at + u] for u in range(UNROLL)]
-                loaded = [wide[pl.ds(2 * row, 2), :] for row in some_rows]
-                for u in range(UNROLL):
-                    picked[side, pl.ds(2 * (at + u), 2), :] = loaded[u]
-
-            repeat(0, tile // UNROLL, some)
-            send[side, k, :, :lanes] = picked[side, pl.ds(0, tile, stride=2), :].astype(BF16)
-            send[side, k, :, lanes:] = picked[side, pl.ds(1, tile, stride=2), :].astype(BF16)
-
-        def chunk(k):
+        def one_tile(k):
             for side in range(2):
-                if CHUNK == 1:
-                    one_tile(side, k)
-                else:
-                    repeat(k * CHUNK, (k + 1) * CHUNK, lambda t: one_tile(side, t))
+                base = (2 * k + side) * tile
+
+                def some(i):
+                    at = i * UNROLL
+                    some_rows = [rows_ref[base + at + u] for u in range(UNROLL)]
+                    loaded = [wide[pl.ds(2 * row, 2), :] for row in some_rows]
+                    for u in range(UNROLL):
+                        picked[side, pl.ds(2 * (at + u), 2), :] = loaded[u]
+
+                repeat(0, tile // UNROLL, some)
+                send[side, k, :, :lanes] = picked[side, pl.ds(0, tile, stride=2), :].astype(BF16)
+                send[side, k, :, lanes:] = picked[side, pl.ds(1, tile, stride=2), :].astype(BF16)
+
+        for k in range(first, last):
+            repeat(sum(CHUNKS[:k]), sum(CHUNKS[: k + 1]), one_tile)
             for side in range(2):
                 halo_copy(layer, side, k).start()
-
-        repeat(first, last, chunk)
 
     def between(value, low, high):
         return jnp.minimum(jnp.maximum(value, low), high)
@@ -275,7 +293,8 @@
             for copy in weight_copies:
                 copy.wait()
         wk_t = wk_ref[layer].T
-        wv, wq = wv_ref[layer], wq_ref[layer]
+        wv, wq, wo = wv_ref[layer], wq_ref[layer], wo_ref[layer]
+        wm = (0.5 * wm_ref[layer].astype(F32)).astype(BF16)
         summ[...] = jnp.zeros_like(summ)
 
         def add_summary(i):
@@ -289,13 +308,16 @@
 
         def ask(i):
             rows = pl.ds(i * ROWS, ROWS)
-            query[rows, :] = feature_map(dot(hidden(i), wq)).astype(BF16)
+            h = hidden(i)
+            query[rows, :] = feature_map(dot(h, wq)).astype(BF16)
+            ahead = dot(h, wm).astype(BF16)
+            lifted[pl.ds(i * some_tiles, some_tiles)] = ahead.reshape(some_tiles, tile, width)
 
 
         def gather_local(i):
             for u in range(GROUP):
                 t = i * GROUP + u
-                tiles_here = [hid[near_ref[t * slots + j]] for j in range(slots)]
+                tiles_here = [lifted[near_ref[t * slots + j]] for j in range(slots)]
                 local[pl.ds(t * tile, tile), :] = dot(
                     blocks_of(t), jnp.concatenate(tiles_here, axis=0)
                 )
@@ -346,18 +368,18 @@
         wait(hop)
         piece[...] = quarter[...] + (r3[layer, 0] + r3[layer, 1] + r3[layer, 2])
 
-        hop = [
-            exchange(layer, k + 6, piece, r4.at[layer, k - 1], z_others[k - 1])
-            for k in range(1, NZ)
-        ]
-        start(hop)
-        gather(layer, SECOND, side_tiles // CHUNK)
+        hop = [exchange(layer, 7, piece, r4.at[layer], z_far)]
+        start(hop)
+        gather(layer, SECOND, THIRD)
         repeat(loops // 4, loops // 2, gather_local)
         wait(hop)
+        coarse[...] = (piece[...] + r4[layer]).astype(BF16)
+        hop = [exchange(layer, 8, coarse, r5.at[layer], z_near)]
+        start(hop)
+        gather(layer, THIRD, len(CHUNKS))
+        wait(hop)
         at = core * (width // 2) + x * share
-        total[layer, pl.ds(at, share), :] = piece[...] + (
-            r4[layer, 0] + r4[layer, 1] + r4[layer, 2]
-        )
+        total[layer, pl.ds(at, share), :] = coarse[...].astype(F32) + r5[layer].astype(F32)
 
         here = total.at[layer, pl.ds(at, share)]
         hop = [
@@ -372,7 +394,6 @@
         repeat(loops // 4 * 3, loops, gather_local)
         wait(hop)
         summary = total[layer].astype(BF16)
-        wo, wm = wo_ref[layer], wm_ref[layer]
         gain = gain_ref[pl.ds(layer, 1), :]
 
         def attend(i):
@@ -384,22 +405,21 @@
 
         repeat(0, steps, attend)
 
-        def arrived(k):
+        for k in range(len(CHUNKS)):
             for side in range(2):
                 halo_copy(layer, side, k).wait()
-
-        repeat(0, side_tiles // CHUNK, arrived)
+                at = pl.ds((1 - side) * side_tiles + sum(CHUNKS[:k]), CHUNKS[k])
+                ahead = dot(halos[layer][at].reshape(CHUNKS[k] * tile, width), wm)
+                halos[layer][at] = ahead.astype(BF16).reshape(CHUNKS[k], tile, width)
 
         def finish_some(first):
             parts_here = []
             for u in range(FINISH // tile):
                 t = first * (FINISH // tile) + u
                 tiles_here = [halos[layer][far_ref[t * slots + j]] for j in range(slots)]
-                both = local[pl.ds(t * tile, tile), :] + dot(
-                    blocks_of(t), jnp.concatenate(tiles_here, axis=0)
-                )
-                parts_here.append(both.astype(BF16))
-            message = silu(dot(jnp.concatenate(parts_here, axis=0), wm))
+                parts_here.append(dot(blocks_of(t), jnp.concatenate(tiles_here, axis=0)))
+            both = local[pl.ds(first * FINISH, FINISH), :] + jnp.concatenate(parts_here, axis=0)
+            message = silu_of_twice(both)
             rows = first * FINISH
             new = keep(rows, res[pl.ds(rows, FINISH), :] + message).astype(BF16)
             at = pl.ds(first * (FINISH // tile), FINISH // tile)
@@ -435,7 +455,6 @@
     layers = w_query.shape[0]
     halo_rows = send_rows.shape[2]
     side_tiles = halo_rows // tile
-    smem = pl.BlockSpec(memory_space=pltpu.SMEM)
     vmem = pl.BlockSpec(memory_space=pltpu.VMEM)
     anywhere = pl.BlockSpec(memory_space=pl.ANY)
     hops = 14
@@ -443,11 +462,12 @@
     out = pl.pallas_call(
         functools.partial(kernel, (layers, vertices, width, tile, slots, halo_rows)),
         out_shape=pltpu.VMEM((tiles, tile, width), BF16),
-        in_specs=[smem] * 4 + [anywhere] * 8,
+        in_specs=[anywhere] * 12,
         out_specs=vmem,
         scratch_shapes=[pltpu.VMEM((layers, width, width), BF16)] * 5
         + [
             pltpu.VMEM((layers, width), F32),
+            pltpu.VMEM((tiles, tile, width), BF16),
             pltpu.VMEM((tiles + 1, tile, width), BF16),
             pltpu.VMEM((2 * side_tiles + 1, tile, width), BF16),
             pltpu.VMEM((2 * side_tiles + 1, tile, width), BF16),
@@ -465,20 +485,27 @@
             pltpu.VMEM((layers, width // 2, width), F32),
             pltpu.VMEM((layers, 3, width // 8, width), F32),
             pltpu.VMEM((layers, 3, width // 8, width), F32),
-            pltpu.VMEM((layers, 3, width // 8, width), F32),
+            pltpu.VMEM((layers, width // 8, width), F32),
+            pltpu.VMEM((layers, width // 8, width), BF16),
+            pltpu.VMEM((width // 8, width), BF16),
             pltpu.VMEM((layers, width, width), F32),
+            pltpu.SMEM((1,), jnp.int32),
+            pltpu.SMEM((2 * halo_rows,), jnp.int32),
+            pltpu.SMEM((slots, tiles), jnp.int32),
+            pltpu.SMEM((tiles,), jnp.int32),
             pltpu.SMEM((tiles * slots,), jnp.int32),
             pltpu.SMEM((tiles * slots,), jnp.int32),
+            pltpu.SemaphoreType.DMA((4,)),
             pltpu.SemaphoreType.DMA((6,)),
             pltpu.SemaphoreType.DMA((vertices // ENTRY_ROWS,)),
             pltpu.SemaphoreType.DMA((BLOCK_COPIES,)),
-            pltpu.SemaphoreType.DMA((2, side_tiles // CHUNK)),
-            pltpu.SemaphoreType.DMA((layers, 2, side_tiles // CHUNK)),
+            pltpu.SemaphoreType.DMA((2, len(CHUNKS))),
+            pltpu.SemaphoreType.DMA((layers, 2, len(CHUNKS))),
             pltpu.SemaphoreType.DMA((layers, hops)),
             pltpu.SemaphoreType.DMA((layers, hops)),
         ],
         compiler_params=pltpu.CompilerParams(
-            collective_id=0, has_side_effects=True, vmem_limit_bytes=58 * 2**20
+            collective_id=0, has_side_effects=True, vmem_limit_bytes=59 * 2**20
         ),
         name="graph_layers",
     )(

time: 115 us -> 111 us (0.965)
  Pallas kernels: 112 us -> 108 us
    pallas_call x1, Pallas kernels: 112 us -> 108 us  [on_device(): pl.pallas_call(functools.partial(kernel, (layers, vertices, width, tile,...]
where the time goes in v5:
time: 111 us; the launch traced here: 110 us
  Pallas kernels  108 us (97%)
  local copies, waits for them, and re-layouts  2.02 us (2%)
    pallas_call x1, Pallas kernels, on_device(): pl.pallas_call(functools.partial(kernel, (layers, vertices, width, tile,...  108 us

profile of v5, /device:TPU:1, one launch (start us, length us, event | category | flops | bytes accessed | tf_op | source)
XLA Modules:
  0.0 110.4 jit_solution(3404144555921106630)
XLA Ops:
  0.7 107.7 %graph_layers.1 = bf16[64,128,256]{2,1,0:T(8,128)(2,1)S(1)} custom-call(s32[1]{0:T(128)S(6)} %copy.16.count_hbm, s32[4096]{0:T(1024)} %bitcast.10, s32[4,64]{1,0:T(4,128)} %bitcast.11, s32[64]{0:T(128)} %used_hbm.1, bf16[64,128,256]{2,1,0:T(8,128)(2,1)} %bitcast.9, bf16[64,4,128,128]{3,2,1,0:T(8,128)(2,1)} %blocks_ref.1, bf16[2,256,256]{2,1,0:T(8,128)(2,1)} %wq_hbm.1, ...), custom_call_target="tpu_custom_call" | custom-call | tf_op jit(solution)/shard_map/graph_layers/pallas_call | solution.py:462
  108.4 2.0 %copy.15 = bf16[8192,256]{1,0:T(8,128)(2,1)} copy(bf16[8192,256]{1,0:T(8,128)(2,1)S(1)} %bitcast.8) | data formatting | bytes 8388608
